TPU v7x, 32 devices: a whole 2x2x4 slice. The times are simulated.
32 devices in a mesh: grp: 4 (over z), cand: 8 (over y, x, core).
Axes of the slice: x: 2, y: 2, z: 4, core: 2. Of those that a mesh axis runs over, the one named last changes fastest.
Arguments:
- embeddings: bfloat16 [96, 1024, 1024], P('grp', 'cand'), may hold values from -6 to 6
- hidden_weight: bfloat16 [2048, 1024], P('cand'), may hold values from -0.1875 to 0.1875
- score_weight: bfloat16 [2048], replicated, may hold values from -0.5 to 0.5
- relevance: int32 [96, 1024], P('grp', 'cand'), may hold values from 0 to 4
- rank_pos: int32 [96, 1024], P('grp', 'cand'), may hold values from 0 to 1023, as said below
- ideal_dcg: float32 [96], P('grp'), may hold values from 32 to 128
Outputs:
- grad_hidden: float32 [2048, 1024], P('cand')
- lambdas: float32 [96, 1024], P('grp', 'cand')
Inputs may be any that keep to these rules, and one draw needn't show every extreme that they name: `rank_pos`: in each group the rank positions are a permutation of 0 to 1023.
All inputs are finite; a program needn't handle non-finite values.
Results may differ from a plain program's by a relative error of at most 0.006.
Values may be sent and summed in bfloat16 or wider, within the bound.
A program may use at most 64 MiB of HBM per device.

v0:
```python
import jax
import jax.numpy as jnp
from jax import lax
from jax.sharding import PartitionSpec as P

EPS = 1e-06


def pair_lambdas(own_score, own_gain, own_disc, far_score, far_gain, far_disc, ideal):
    gain_diff = far_gain[..., None, :] - own_gain[..., :, None]
    toward = jnp.sign(gain_diff)
    weight = (
        jnp.abs(gain_diff)
        * jnp.abs(far_disc[..., None, :] - own_disc[..., :, None])
        / ideal[..., None, None]
    )
    margin = own_score[..., :, None] - far_score[..., None, :]
    return jnp.sum(weight * toward * jax.nn.sigmoid(toward * margin), axis=-1)


def gain_of(labels):
    return jnp.exp2(labels.astype(jnp.float32)) - 1.0


def discount_of(positions):
    return 1.0 / jnp.log2(2.0 + positions.astype(jnp.float32))


def per_device(embeddings, hidden_weight, score_weight, relevance, rank_pos, ideal_dcg):
    grp_count, local, width = embeddings.shape
    cand_rows = embeddings.reshape(grp_count * local, width)
    pre_act = lax.dot_general(
        cand_rows,
        lax.all_gather(hidden_weight, "cand", axis=0, tiled=True),
        (((1,), (1,)), ((), ())),
        preferred_element_type=jnp.float32,
    )
    acts, pull = jax.vjp(jax.nn.gelu, pre_act)
    scores = jnp.dot(
        acts.astype(jnp.bfloat16), score_weight, preferred_element_type=jnp.float32
    ).reshape(grp_count, local)
    gain_vals = gain_of(relevance)
    discount = discount_of(rank_pos)
    lambdas = pair_lambdas(
        scores,
        gain_vals,
        discount,
        lax.all_gather(scores, "cand", axis=1, tiled=True),
        lax.all_gather(gain_vals, "cand", axis=1, tiled=True),
        lax.all_gather(discount, "cand", axis=1, tiled=True),
        ideal_dcg,
    )
    upstream = (
        lambdas.reshape(grp_count * local)[:, None] * score_weight.astype(jnp.float32)[None, :]
    )
    grad_pre = pull(upstream)[0].astype(jnp.bfloat16)
    owned = lax.psum_scatter(
        lax.dot_general(
            grad_pre, cand_rows, (((0,), (0,)), ((), ())), preferred_element_type=jnp.float32
        ).astype(jnp.bfloat16),
        "cand",
        scatter_dimension=0,
        tiled=True,
    ).astype(jnp.float32)
    summed = lax.psum(owned, "grp")
    squares = lax.psum(jnp.sum(summed * summed), "cand")
    entries = summed.shape[0] * summed.shape[1] * lax.axis_size("cand")
    scale = lax.rsqrt(squares / entries + EPS)
    return (summed * scale, lambdas)


def solution(mesh):
    return jax.shard_map(
        per_device,
        mesh=mesh,
        in_specs=(
            P("grp", "cand", None),
            P("cand", None),
            P(),
            P("grp", "cand"),
            P("grp", "cand"),
            P("grp"),
        ),
        out_specs=(P("cand", None), P("grp", "cand")),
        check_vma=False,
    )
```

profile of v0, /device:TPU:0, one launch (start us, length us, event | category | flops | bytes accessed | tf_op | source)
XLA Modules:
  0.0 254.7 jit_solution(1957202030902142692)
XLA Ops:
  7.2 0.0 all-gather.2.cloned.1.call-start
  7.2 0.7 all-gather.2.cloned.1.call-update
  7.9 0.0 reduce-scatter.2.cloned.1.call-start
  7.9 0.7 reshape.18
  8.6 0.7 convert_element_type.24
  9.3 0.7 exponential_add_fusion
  10.0 10.7 %all_gather.12 = f32[24,1024]{1,0:T(8,128)S(1)} all-gather(f32[24,128]{1,0:T(8,128)S(1)} %exponential_add_fusion), channel_id=1, replica_groups=mesh['grp'=4,'cand'=8] {'cand'}, dimensions={1}, use_global_device_ids=true | all-gather | bytes 110592 | tf_op jit(solution)/shard_map/all_gather | solution.py:49
  20.7 0.7 multiply_divide_fusion
  21.5 9.5 %all_gather.13 = f32[24,1024]{1,0:T(8,128)S(1)} all-gather(f32[24,128]{1,0:T(8,128)S(1)} %multiply_divide_fusion), channel_id=1, replica_groups=mesh['grp'=4,'cand'=8] {'cand'}, dimensions={1}, use_global_device_ids=true | all-gather | bytes 110592 | tf_op jit(solution)/shard_map/all_gather | solution.py:50
  31.0 18.5 %all-gather.2.cloned.1.call-done = bf16[2048,1024]{1,0:T(8,128)(2,1)} async-done(((bf16[256,1024]{1,0:T(8,128)(2,1)}), bf16[2048,1024]{1,0:T(8,128)(2,1)}) %all-gather.2.cloned.1.call-update) | async-done | bytes 4194320 | tf_op jit(solution)/shard_map/all_gather | solution.py:34
  49.5 19.7 %fusion.36 = f32[3072,2048]{1,0:T(8,128)} fusion(bf16[3072,1024]{1,0:T(8,128)(2,1)} %bitcast.11, bf16[2048,1024]{1,0:T(8,128)(2,1)} %all-gather.2.cloned.1.call-done), kind=kOutput, calls=%fused_computation.44 | convolution fusion | flops 12884901888 | bytes 35651584 | tf_op jit(solution)/shard_map/dot_general | solution.py:32
  69.1 0.0 copy-start
  69.1 11.9 %fusion.20 = f32[1,3072]{1,0:T(1,128)S(1)} fusion(bf16[2048,1]{0,1:T(2,128)(2,1)S(1)} %reshape.18, f32[3072,2048]{1,0:T(8,128)} %fusion.36), kind=kOutput, calls=%fused_computation.27 | convolution fusion | flops 69206016 | bytes 25182208 | tf_op jit(solution)/shard_map/dot_general | solution.py:39
  81.1 9.1 %all_gather.15 = f32[24,1024]{1,0:T(8,128)S(1)} all-gather(f32[24,128]{1,0:T(8,128)S(1)} %bitcast.9), channel_id=1, replica_groups=mesh['grp'=4,'cand'=8] {'cand'}, dimensions={1}, use_global_device_ids=true | all-gather | bytes 110592 | tf_op jit(solution)/shard_map/all_gather | solution.py:48
  90.2 0.0 copy-done
  90.2 11.2 %fusion.13 = f32[24,128]{1,0:T(8,128)S(1)} fusion(f32[24,1024]{1,0:T(8,128)S(1)} %all_gather.15, f32[24,128]{1,0:T(8,128)S(1)} %bitcast.10, f32[24]{0:T(128)S(1)} %copy-done, f32[24,128]{1,0:T(8,128)S(1)} %multiply_divide_fusion, f32[24,1024]{1,0:T(8,128)S(1)} %all_gather.13, f32[24,128]{1,0:T(8,128)S(1)} %exponential_add_fusion, f32[24,1024]{1,0:T(8,128)S(1)} %all_gather.12), kind=kLoop, calls=%fused_computation.20 | loop fusion | flops 47182848 | bytes 344160 | tf_op jit(solution)/shard_map/reduce_sum | solution.py:18
  101.4 0.0 copy-start.1
  101.4 35.9 %fusion.23 = bf16[2048,1024]{1,0:T(8,128)(2,1)} fusion(bf16[3072,1024]{1,0:T(8,128)(2,1)} %bitcast.12, f32[3072,2048]{1,0:T(8,128)} %fusion.36, f32[2048]{0:T(1024)S(1)} %convert_element_type.24, f32[3072]{0:T(1024)S(1)} %bitcast.13), kind=kOutput, calls=%fused_computation.29 | convolution fusion | flops 13019119616 | bytes 35672064 | tf_op jit(solution)/shard_map/dot_general | solution.py:58
  137.3 0.0 copy-done.1
  137.3 0.0 reduce-scatter.2.cloned.1.call-update
  137.4 51.3 %reduce-scatter.2.cloned.1.call-done = bf16[256,1024]{1,0:T(8,128)(2,1)} async-done(((bf16[2048,1024]{1,0:T(8,128)(2,1)}), bf16[256,1024]{1,0:T(8,128)(2,1)}) %reduce-scatter.2.cloned.1.call-update) | async-done | bytes 524304 | tf_op jit(solution)/shard_map/reduce_scatter | solution.py:57
  188.7 44.2 %all-reduce.1 = f32[256,1024]{1,0:T(8,128)S(1)} all-reduce(bf16[256,1024]{1,0:T(8,128)(2,1)} %reduce-scatter.2.cloned.1.call-done), channel_id=1, replica_groups=mesh['grp'=4,'cand'=8] {'grp'}, use_global_device_ids=true, to_apply=%region_2.0 | all-reduce | flops 262144 | bytes 1572864 | tf_op jit(solution)/shard_map/psum | solution.py:65
  232.9 0.9 multiply_reduce_fusion
  233.8 12.4 %psum.15 = f32[]{:T(128)} all-reduce(f32[]{:T(128)} %multiply_reduce_fusion), channel_id=1, replica_groups=mesh['grp'=4,'cand'=8] {'cand'}, use_global_device_ids=true, to_apply=%region_4.0 | all-reduce | flops 1 | bytes 8 | tf_op jit(solution)/shard_map/psum | solution.py:66
  246.9 1.0 broadcast_multiply_fusion
Async XLA Ops:
  7.2 42.3 %all-gather.2.cloned.1.call-start = ((), (), s32[]{:S(2)}) async-start(), calls=%async_computation.1 | async-start | bytes 4718592 | tf_op jit(solution)/shard_map/all_gather | solution.py:34
  7.9 180.8 %reduce-scatter.2.cloned.1.call-start = ((), (), s32[]{:S(2)}) async-start(), calls=%async_computation.2 | async-start | bytes 4718592 | tf_op jit(solution)/shard_map/reduce_scatter | solution.py:57
  69.1 21.1 %copy-start = (f32[24]{0:T(128)S(1)}, f32[24]{0:T(128)}, u32[]{:S(2)}) copy-start(f32[24]{0:T(128)} %param.11) | copy-start | bytes 292
  101.4 36.0 %copy-start.1 = (f32[24,128]{1,0:T(8,128)}, f32[24,128]{1,0:T(8,128)S(1)}, u32[]{:S(2)}) copy-start(f32[24,128]{1,0:T(8,128)S(1)} %fusion.13) | copy-start | bytes 36868
Sparse Core Ops, SparseCore 0:
  9.9 39.5 all-gather.1
  137.5 51.1 reduce-scatter.1
where the time goes:
time: 255 us
  blocking collectives  86 us (34%)
  waiting for transfers between devices  70.5 us (28%)
  matrix products  67.5 us (26%)
  other arithmetic  15.2 us (6%)
  between operations  14.8 us (6%)
    reduce_scatter x1, waiting for transfers between devices, per_device(): lax.psum_scatter(lax.dot_general(grad_pre, cand_rows, (((0,), (0,)), ((),...  51.3 us
    psum x1, blocking collectives, per_device(): summed = lax.psum(owned, 'grp')  44.2 us
    dot_general x1, matrix products, per_device(): lax.dot_general(grad_pre, cand_rows, (((0,), (0,)), ((), ())), preferred_...  35.9 us
    dot_general x1, matrix products, per_device(): lax.dot_general(cand_rows, lax.all_gather(hidden_weight, 'cand', axis=0,...  19.7 us
    all_gather x1, waiting for transfers between devices, per_device(): lax.all_gather(hidden_weight, 'cand', axis=0, tiled=True)  18.5 us
    psum x1, blocking collectives, per_device(): squares = lax.psum(jnp.sum(summed * summed), 'cand')  12.4 us
    dot_general x1, matrix products, per_device(): jnp.dot(acts.astype(jnp.bfloat16), score_weight, preferred_element_type=j...  11.9 us
    reduce_sum x1, other arithmetic, pair_lambdas(): return jnp.sum(weight * toward * jax.nn.sigmoid(toward * margin), axis=-1)  11.2 us
  transfers between devices with their start and end apart: 2, of which 2 were waited for; matrix products, arithmetic and copies ran while one was open for 1% of the time, Pallas kernels for 0%

commit v1 on v0

--- a/solution.py
+++ b/solution.py
@@ -62,7 +62,9 @@
         scatter_dimension=0,
         tiled=True,
     ).astype(jnp.float32)
-    summed = lax.psum(owned, "grp")
+    summed = owned
+    for hop in (1, 2):
+        summed = summed + lax.ppermute(summed, "grp", [(dev, dev ^ hop) for dev in range(4)])
     squares = lax.psum(jnp.sum(summed * summed), "cand")
     entries = summed.shape[0] * summed.shape[1] * lax.axis_size("cand")
     scale = lax.rsqrt(squares / entries + EPS)

time: 255 us -> 286 us (1.12)
  waiting for transfers between devices: 70.5 us -> 139 us
  blocking collectives: 86 us -> 41.9 us
  starting transfers between devices: 0.08 us -> 4.11 us
    ppermute x0 -> x2, waiting for transfers between devices: none -> 68.1 us  [per_device(): lax.ppermute(summed, 'grp', [(dev, dev ^ hop) for dev in range(4)])]
    psum x1 -> x0, blocking collectives: 44.2 us -> none  [per_device(): summed = lax.psum(owned, 'grp')]
    ppermute x0 -> x2, starting transfers between devices: none -> 4.03 us  [per_device(): lax.ppermute(summed, 'grp', [(dev, dev ^ hop) for dev in range(4)])]
  transfers between devices with their start and end apart: 2 -> 4, of which waited for: 2 -> 4; matrix products, arithmetic and copies ran while one was open for 1% -> 1% of each run, Pallas kernels for 0% -> 0%
where the time goes in v1:
time: 286 us; the launch traced here: 285 us
  waiting for transfers between devices  139 us (49%)
  matrix products  67.5 us (24%)
  blocking collectives  41.9 us (15%)
  other arithmetic  17.7 us (6%)
  between operations  14.8 us (5%)
  starting transfers between devices  4.11 us (1%)
    ppermute x2, waiting for transfers between devices, per_device(): lax.ppermute(summed, 'grp', [(dev, dev ^ hop) for dev in range(4)])  68.1 us
    reduce_scatter x1, waiting for transfers between devices, per_device(): lax.psum_scatter(lax.dot_general(grad_pre, cand_rows, (((0,), (0,)), ((),...  51.3 us
    dot_general x1, matrix products, per_device(): lax.dot_general(grad_pre, cand_rows, (((0,), (0,)), ((), ())), preferred_...  35.9 us
    dot_general x1, matrix products, per_device(): lax.dot_general(cand_rows, lax.all_gather(hidden_weight, 'cand', axis=0,...  19.7 us
    all_gather x1, waiting for transfers between devices, per_device(): lax.all_gather(hidden_weight, 'cand', axis=0, tiled=True)  18.5 us
    psum x1, blocking collectives, per_device(): squares = lax.psum(jnp.sum(summed * summed), 'cand')  12.6 us
    dot_general x1, matrix products, per_device(): jnp.dot(acts.astype(jnp.bfloat16), score_weight, preferred_element_type=j...  11.9 us
    reduce_sum x1, other arithmetic, pair_lambdas(): return jnp.sum(weight * toward * jax.nn.sigmoid(toward * margin), axis=-1)  11.2 us
  transfers between devices with their start and end apart: 4, of which 4 were waited for; matrix products, arithmetic and copies ran while one was open for 1% of the time, Pallas kernels for 0%

profile of v1, /device:TPU:0, one launch (start us, length us, event | category | flops | bytes accessed | tf_op | source)
XLA Modules:
  0.0 285.3 jit_solution(2072965509809762156)
XLA Ops:
  7.2 0.0 all-gather.2.cloned.1.call-start
  7.2 0.7 all-gather.2.cloned.1.call-update
  7.9 0.0 reduce-scatter.2.cloned.1.call-start
  7.9 0.7 reshape.18
  8.6 0.7 convert_element_type.24
  9.3 0.7 exponential_add_fusion
  10.0 10.7 %all_gather.12 = f32[24,1024]{1,0:T(8,128)S(1)} all-gather(f32[24,128]{1,0:T(8,128)S(1)} %exponential_add_fusion), channel_id=1, replica_groups=mesh['grp'=4,'cand'=8] {'cand'}, dimensions={1}, use_global_device_ids=true | all-gather | bytes 110592 | tf_op jit(solution)/shard_map/all_gather | solution.py:49
  20.7 0.7 multiply_divide_fusion
  21.5 9.5 %all_gather.13 = f32[24,1024]{1,0:T(8,128)S(1)} all-gather(f32[24,128]{1,0:T(8,128)S(1)} %multiply_divide_fusion), channel_id=1, replica_groups=mesh['grp'=4,'cand'=8] {'cand'}, dimensions={1}, use_global_device_ids=true | all-gather | bytes 110592 | tf_op jit(solution)/shard_map/all_gather | solution.py:50
  31.0 18.5 %all-gather.2.cloned.1.call-done = bf16[2048,1024]{1,0:T(8,128)(2,1)} async-done(((bf16[256,1024]{1,0:T(8,128)(2,1)}), bf16[2048,1024]{1,0:T(8,128)(2,1)}) %all-gather.2.cloned.1.call-update) | async-done | bytes 4194320 | tf_op jit(solution)/shard_map/all_gather | solution.py:34
  49.5 19.7 %fusion.36 = f32[3072,2048]{1,0:T(8,128)} fusion(bf16[3072,1024]{1,0:T(8,128)(2,1)} %bitcast.11, bf16[2048,1024]{1,0:T(8,128)(2,1)} %all-gather.2.cloned.1.call-done), kind=kOutput, calls=%fused_computation.45 | convolution fusion | flops 12884901888 | bytes 35651584 | tf_op jit(solution)/shard_map/dot_general | solution.py:32
  69.1 0.0 copy-start
  69.1 11.9 %fusion.20 = f32[1,3072]{1,0:T(1,128)S(1)} fusion(bf16[2048,1]{0,1:T(2,128)(2,1)S(1)} %reshape.18, f32[3072,2048]{1,0:T(8,128)} %fusion.36), kind=kOutput, calls=%fused_computation.27 | convolution fusion | flops 69206016 | bytes 25182208 | tf_op jit(solution)/shard_map/dot_general | solution.py:39
  81.1 9.1 %all_gather.15 = f32[24,1024]{1,0:T(8,128)S(1)} all-gather(f32[24,128]{1,0:T(8,128)S(1)} %bitcast.9), channel_id=1, replica_groups=mesh['grp'=4,'cand'=8] {'cand'}, dimensions={1}, use_global_device_ids=true | all-gather | bytes 110592 | tf_op jit(solution)/shard_map/all_gather | solution.py:48
  90.2 0.0 copy-done
  90.2 11.2 %fusion.13 = f32[24,128]{1,0:T(8,128)S(1)} fusion(f32[24,1024]{1,0:T(8,128)S(1)} %all_gather.15, f32[24,128]{1,0:T(8,128)S(1)} %bitcast.10, f32[24]{0:T(128)S(1)} %copy-done, f32[24,128]{1,0:T(8,128)S(1)} %multiply_divide_fusion, f32[24,1024]{1,0:T(8,128)S(1)} %all_gather.13, f32[24,128]{1,0:T(8,128)S(1)} %exponential_add_fusion, f32[24,1024]{1,0:T(8,128)S(1)} %all_gather.12), kind=kLoop, calls=%fused_computation.20 | loop fusion | flops 47182848 | bytes 344160 | tf_op jit(solution)/shard_map/reduce_sum | solution.py:18
  101.4 0.0 copy-start.1
  101.4 35.9 %fusion.23 = bf16[2048,1024]{1,0:T(8,128)(2,1)} fusion(bf16[3072,1024]{1,0:T(8,128)(2,1)} %bitcast.12, f32[3072,2048]{1,0:T(8,128)} %fusion.36, f32[2048]{0:T(1024)S(1)} %convert_element_type.24, f32[3072]{0:T(1024)S(1)} %bitcast.13), kind=kOutput, calls=%fused_computation.29 | convolution fusion | flops 13019119616 | bytes 35672064 | tf_op jit(solution)/shard_map/dot_general | solution.py:58
  137.3 0.0 copy-done.1
  137.3 0.0 reduce-scatter.2.cloned.1.call-update
  137.4 51.3 %reduce-scatter.2.cloned.1.call-done = bf16[256,1024]{1,0:T(8,128)(2,1)} async-done(((bf16[2048,1024]{1,0:T(8,128)(2,1)}), bf16[256,1024]{1,0:T(8,128)(2,1)}) %reduce-scatter.2.cloned.1.call-update) | async-done | bytes 524304 | tf_op jit(solution)/shard_map/reduce_scatter | solution.py:57
  188.7 1.1 convert_element_type.27
  189.8 1.5 collective-permute-start
  191.4 23.2 %collective-permute-done = f32[256,1024]{1,0:T(8,128)S(1)} collective-permute-done((f32[256,1024]{1,0:T(8,128)S(1)}, f32[256,1024]{1,0:T(8,128)S(1)}, u32[]{:S(2)}, u32[]{:S(2)}) %collective-permute-start) | collective-permute-done | bytes 1048608 | tf_op jit(solution)/shard_map/ppermute | solution.py:67
  214.6 1.2 convert_add_fusion
  215.8 2.5 collective-permute-start.1
  218.3 44.8 %collective-permute-done.1 = f32[256,1024]{1,0:T(8,128)S(1)} collective-permute-done((f32[256,1024]{1,0:T(8,128)S(1)}, f32[256,1024]{1,0:T(8,128)S(1)}, u32[]{:S(2)}, u32[]{:S(2)}) %collective-permute-start.1) | collective-permute-done | bytes 1048608 | tf_op jit(solution)/shard_map/ppermute | solution.py:67
  263.1 1.0 multiply_reduce_fusion
  264.1 12.6 %psum.7 = f32[]{:T(128)} all-reduce(f32[]{:T(128)} %get-tuple-element.2), channel_id=1, replica_groups=mesh['grp'=4,'cand'=8] {'cand'}, use_global_device_ids=true, to_apply=%region_3.0 | all-reduce | flops 1 | bytes 8 | tf_op jit(solution)/shard_map/psum | solution.py:68
  277.4 1.0 broadcast_multiply_fusion
Async XLA Ops:
  7.2 42.3 %all-gather.2.cloned.1.call-start = ((), (), s32[]{:S(2)}) async-start(), calls=%async_computation.1 | async-start | bytes 4718592 | tf_op jit(solution)/shard_map/all_gather | solution.py:34
  7.9 180.8 %reduce-scatter.2.cloned.1.call-start = ((), (), s32[]{:S(2)}) async-start(), calls=%async_computation.2 | async-start | bytes 4718592 | tf_op jit(solution)/shard_map/reduce_scatter | solution.py:57
  69.1 21.1 %copy-start = (f32[24]{0:T(128)S(1)}, f32[24]{0:T(128)}, u32[]{:S(2)}) copy-start(f32[24]{0:T(128)} %param.11) | copy-start | bytes 292
  101.4 36.0 %copy-start.1 = (f32[24,128]{1,0:T(8,128)}, f32[24,128]{1,0:T(8,128)S(1)}, u32[]{:S(2)}) copy-start(f32[24,128]{1,0:T(8,128)S(1)} %fusion.13) | copy-start | bytes 36868
  189.8 24.8 %collective-permute-start = (f32[256,1024]{1,0:T(8,128)S(1)}, f32[256,1024]{1,0:T(8,128)S(1)}, u32[]{:S(2)}, u32[]{:S(2)}) collective-permute-start(f32[256,1024]{1,0:T(8,128)S(1)} %convert_element_type.27), channel_id=1, source_target_pairs={{0,8},{8,0},{16,24},{24,16},{1,9},{9,1},{17,25},{25,17},{2,10},{10... | collective-permute-start | bytes 3145736 | tf_op jit(solution)/shard_map/ppermute | solution.py:67
  215.8 47.3 %collective-permute-start.1 = (f32[256,1024]{1,0:T(8,128)S(1)}, f32[256,1024]{1,0:T(8,128)S(1)}, u32[]{:S(2)}, u32[]{:S(2)}) collective-permute-start(f32[256,1024]{1,0:T(8,128)S(1)} %convert_add_fusion), channel_id=1, source_target_pairs={{0,16},{8,24},{16,0},{24,8},{1,17},{9,25},{17,1},{25,9},{2,18},{10... | collective-permute-start | bytes 3145736 | tf_op jit(solution)/shard_map/ppermute | solution.py:67
Sparse Core Ops, SparseCore 0:
  9.9 39.5 all-gather.1
  137.5 51.1 reduce-scatter.1
